TPU v7x, 32 devices: a whole 2x2x4 slice. The times are simulated.
32 devices in a mesh: scene: 2 (over y), cam: 16 (over z, x, core).
Axes of the slice: x: 2, y: 2, z: 4, core: 2. Of those that a mesh axis runs over, the one named last changes fastest.
Arguments:
- queries: bfloat16 [32, 768, 1024], P(('scene', 'cam')), parts along dimension 0, may hold values from -32 to 32
- keys: bfloat16 [32, 768, 1024], P(('scene', 'cam')), parts along dimension 0, may hold values from -32 to 32
- values: bfloat16 [32, 768, 1024], P(('scene', 'cam')), parts along dimension 0, may hold values from -6 to 6
- residual: bfloat16 [32, 768, 1024], P(('scene', 'cam')), parts along dimension 0, may hold values from -1.5 to 1.5
- w_out: bfloat16 [1024, 1024], replicated, may hold values from -0.1875 to 0.1875
- neighbours: int32 [32, 4], P(('scene', 'cam')), parts along dimension 0, may hold values from 0 to 15, as said below
- band_start: int32 [32, 4], P(('scene', 'cam')), parts along dimension 0, may hold values from 0 to 3
- band_blocks: int32 [32, 4, 6, 2], P(('scene', 'cam')), parts along dimension 0, may hold values from 0 to 2, as said below
- band_count: int32 [32, 4, 6], P(('scene', 'cam')), parts along dimension 0, may hold values from 1 to 2, as said below
Outputs:
- output: bfloat16 [32, 768, 1024], P(('scene', 'cam')), parts along dimension 0
There are 2 independent parts, one for each index of `scene`. A program takes and returns all parts, laid end to end along the dimension named above; an argument that names none is the same for every part. Nothing has to cross between parts.
Inputs may be any that keep to these rules, and one draw needn't show every extreme that they name: `neighbours`: row v lists the views (v + k) mod 16 for k = 1, -1, 2, -2, each once, in an order drawn for each row. `band_blocks`: each list holds 2 different numbers; entries at positions band_count or later are not read. `band_count`: query block 0 of every slot has 2.
All inputs are finite; a program needn't handle non-finite values.
Results may differ from a plain program's by a relative error of at most 0.008.
Values may be sent and summed in bfloat16 or wider, within the bound.
A program may use at most 128 MiB of HBM per device.

v0:
```python
import math

import jax
import jax.numpy as jnp
from jax import lax
from jax.sharding import PartitionSpec as P

HEADS = 16


def passed_along(block, axis, distance):
    devices = range(lax.axis_size(axis))
    route = [((i - distance) % len(devices), i) for i in devices]
    return lax.ppermute(block, axis, route)


def shortened(x):

    def short(part):
        return part.astype(jnp.bfloat16) if part.dtype == jnp.float32 else part

    return jax.tree.map(short, x)


def per_device(
    queries, keys, values, residual, w_out, neighbours, band_start, band_blocks, band_count
):
    query_rows = queries[0]
    key_rows = keys[0]
    value_rows = values[0]
    tokens, model_width = query_rows.shape
    qblocks = band_count.shape[2]
    most_blocks = band_blocks.shape[3]
    block_len = tokens // qblocks
    window_blocks = max(2, qblocks // 2)
    head_dim = model_width // HEADS
    score_scale = 1.0 / math.sqrt(head_dim)
    cameras = lax.axis_size("cam")
    rig_count = cameras // min(32, cameras)
    self_index = lax.axis_index("cam")
    offsets = (1, -1, 2, -2)

    def cycle_of(offset):
        return (self_index + offset * rig_count + 2 * cameras) % cameras

    source_cams = jnp.stack([cycle_of(-offset) for offset in offsets])
    slot_match = (neighbours[0][None, :] == source_cams[:, None]).astype(jnp.int32)
    slot_starts = jnp.sum(slot_match * band_start[0][None, :], axis=1)
    relative = jnp.sum(slot_match[:, :, None, None] * band_blocks[0][None], axis=1)
    slot_count = jnp.sum(slot_match[:, :, None] * band_count[0][None], axis=1)

    def asked_start(position):
        offset = offsets[position]
        wanted = lax.dynamic_slice_in_dim(slot_starts, position, 1, 0)
        return passed_along(wanted, "cam", -offset * rig_count)

    def band_slice(position):
        first_block = asked_start(position)[0]
        return (
            lax.dynamic_slice_in_dim(
                key_rows, first_block * block_len, window_blocks * block_len, 0
            ),
            lax.dynamic_slice_in_dim(
                value_rows, first_block * block_len, window_blocks * block_len, 0
            ),
        )

    near_prev = passed_along(shortened(band_slice(0)), "cam", rig_count)
    near_next = passed_along(shortened(band_slice(1)), "cam", -rig_count)
    far_prev = passed_along(shortened(band_slice(2)), "cam", 2 * rig_count)
    far_next = passed_along(shortened(band_slice(3)), "cam", -2 * rig_count)
    received = (near_prev, near_next, far_prev, far_next)
    key_tiles = [buffer[0].reshape(-1, block_len, model_width) for buffer in received]
    value_tiles = [buffer[1].reshape(-1, block_len, model_width) for buffer in received]
    own_queries = query_rows.reshape(qblocks, block_len, HEADS, head_dim)
    own_keys = key_rows.reshape(qblocks, block_len, model_width)
    own_values = value_rows.reshape(qblocks, block_len, model_width)
    group_size = math.gcd(qblocks, max(1, 512 // block_len))
    group_count = qblocks // group_size

    def one_group(turn_index):
        first_block = turn_index * group_size
        query_group = lax.dynamic_slice_in_dim(own_queries, first_block, group_size, 0)
        key_parts = [lax.dynamic_slice_in_dim(own_keys, first_block, group_size, 0)]
        value_parts = [lax.dynamic_slice_in_dim(own_values, first_block, group_size, 0)]
        mask_parts = [jnp.ones((group_size, block_len), dtype=bool)]
        for source in range(4):
            block_index = lax.dynamic_slice_in_dim(relative[source], first_block, group_size, 0)
            key_parts.append(
                key_tiles[source][block_index].reshape(
                    group_size, most_blocks * block_len, model_width
                )
            )
            value_parts.append(
                value_tiles[source][block_index].reshape(
                    group_size, most_blocks * block_len, model_width
                )
            )
            live_count = lax.dynamic_slice_in_dim(slot_count[source], first_block, group_size, 0)
            live_slots = jnp.arange(most_blocks, dtype=jnp.int32)[None, :] < live_count[:, None]
            mask_parts.append(jnp.repeat(live_slots, block_len, axis=1))
        key_group = jnp.concatenate(key_parts, axis=1).reshape(group_size, -1, HEADS, head_dim)
        value_group = jnp.concatenate(value_parts, axis=1).reshape(group_size, -1, HEADS, head_dim)
        visible = jnp.concatenate(mask_parts, axis=1)
        scores = (
            jnp.einsum(
                "gqhd,gkhd->ghqk", query_group, key_group, preferred_element_type=jnp.float32
            )
            * score_scale
        )
        scores = jnp.where(visible[:, None, None, :], scores, -jnp.inf)
        row_max = jnp.max(scores, axis=-1, keepdims=True)
        expo_scores = jnp.exp(scores - row_max)
        weights = (expo_scores / jnp.sum(expo_scores, axis=-1, keepdims=True)).astype(jnp.bfloat16)
        mixed_rows = jnp.einsum(
            "ghqk,gkhd->gqhd", weights, value_group, preferred_element_type=jnp.float32
        )
        return mixed_rows.astype(jnp.bfloat16).reshape(group_size * block_len, model_width)

    attended = lax.map(one_group, jnp.arange(group_count, dtype=jnp.int32)).reshape(
        tokens, model_width
    )
    result_rows = residual[0].astype(jnp.float32) + jnp.dot(
        attended, w_out, preferred_element_type=jnp.float32
    )
    return result_rows.astype(jnp.bfloat16)[None]


def solution(mesh):
    return jax.shard_map(
        per_device,
        mesh=mesh,
        in_specs=(
            P(("scene", "cam"), None, None),
            P(("scene", "cam"), None, None),
            P(("scene", "cam"), None, None),
            P(("scene", "cam"), None, None),
            P(),
            P(("scene", "cam"), None),
            P(("scene", "cam"), None),
            P(("scene", "cam"), None, None, None),
            P(("scene", "cam"), None, None),
        ),
        out_specs=P(("scene", "cam"), None, None),
        check_vma=False,
    )
```

profile of v0, /device:TPU:31, one launch (start us, length us, event | category | flops | bytes accessed | tf_op | source)
XLA Modules:
  0.0 504.0 jit_solution(16971063949819060281)
XLA Ops:
  3.2 3.7 collective-permute-start.2
  8.9 4.0 collective-permute-done
  16.2 4.4 collective-permute-start.8
  23.8 34.9 %collective-permute-done.11 = bf16[384,1024]{1,0:T(8,128)(2,1)} collective-permute-done((bf16[384,1024]{1,0:T(8,128)(2,1)S(1)}, bf16[384,1024]{1,0:T(8,128)(2,1)}, u32[]{:S(2)}, u32[]{:S(2)}) %collective-permute-start.11) | collective-permute-done | bytes 786464 | tf_op jit(solution)/shard_map/ppermute | solution.py:14
  58.8 4.4 collective-permute-start.1
  63.2 20.4 %collective-permute-start.5 = (bf16[384,1024]{1,0:T(8,128)(2,1)}, bf16[384,1024]{1,0:T(8,128)(2,1)}, u32[]{:S(2)}, u32[]{:S(2)}) collective-permute-start(bf16[384,1024]{1,0:T(8,128)(2,1)} %get-tuple-element.195), channel_id=1, source_target_pairs={{14,0},{15,1},{0,2},{1,3},{2,4},{3,5},{4,6},{5,7},{6,8},{7,9},{8,1... | collective-permute-start | bytes 2359304 | tf_op jit(solution)/shard_map/ppermute | solution.py:14
  83.9 5.2 %reshape.376 = bf16[6,128,16,64]{3,2,1,0:T(8,128)(2,1)} reshape(bf16[1,768,1024]{2,1,0:T(8,128)(2,1)} %param.11) | data formatting | bytes 3145728 | tf_op jit(solution)/shard_map/reshape;squeeze | solution.py:75
  89.1 4.9 copy.80
  94.2 5.8 %collective-permute-done.10 = bf16[384,1024]{1,0:T(8,128)(2,1)} collective-permute-done((bf16[384,1024]{1,0:T(8,128)(2,1)S(1)}, bf16[384,1024]{1,0:T(8,128)(2,1)}, u32[]{:S(2)}, u32[]{:S(2)}) %collective-permute-start.10) | collective-permute-done | bytes 786464 | tf_op jit(solution)/shard_map/ppermute | solution.py:14
  100.0 19.2 %collective-permute-done.5 = bf16[384,1024]{1,0:T(8,128)(2,1)} collective-permute-done((bf16[384,1024]{1,0:T(8,128)(2,1)}, bf16[384,1024]{1,0:T(8,128)(2,1)}, u32[]{:S(2)}, u32[]{:S(2)}) %collective-permute-start.5) | collective-permute-done | bytes 786464 | tf_op jit(solution)/shard_map/ppermute | solution.py:14
  119.2 380.0 %while.10 = (s32[]{:T(128)}, bf16[3,256,1024]{2,1,0:T(8,128)(2,1)}, s32[3]{0:T(128)S(1)}, bf16[6,128,1024]{2,1,0:T(8,128)(2,1)}, s32[4,6,2]{2,1,0:T(8,128)S(1)},...) while((s32[]{:T(128)}, bf16[3,256,1024]{2,1,0:T(8,128)(2,1)}, ...), condition=%wide.region_6.7_spmd, body=%wide.region_3.6_spmd.sunk | while | flops 1236538624 | bytes 166787424 | solution.py:120
  128.4 2.8 copy.137
  131.2 4.0 reshape.431
  135.3 3.5 copy.142
  144.2 4.0 reshape.426
  148.3 3.5 copy.138
  151.8 4.0 reshape.432
  155.9 3.6 copy.143
  164.9 4.0 reshape.428
  168.9 3.5 copy.139
  172.4 4.0 reshape.433
  176.5 3.6 copy.144
  180.1 2.8 gather_fusion.7
  185.6 4.0 reshape.430
  189.6 3.5 copy.140
  193.2 4.0 reshape.434
  197.2 3.6 copy.145
  217.1 11.1 %fusion.58 = (f32[2,16,128]{2,1,0:T(8,128)S(1)}, f32[2,16,128,1152]{3,2,1,0:T(8,128)}) fusion(pred[2,1152]{1,0:T(4,128)(4,1)S(1)} %constant_dynamic-update-slice_fusion.41, bf16[2,1152,16,64]{1,3,2,0:T(8,128)(2,1)} %copy-done.8, bf16[6,128,16,64]{1,3,2,0:T(8,128)(2,1)} %get-tuple-element.387, s32[]{:T(128)S(6)} %select_n.121), kind=kOutput, calls=%fused_computation.97.clone.1 | convolution fusion | flops 622855296 | bytes 24135940 | tf_op jit(solution)/shard_map/while/body/eval_jaxpr/sub | solution.py:113
  228.2 12.4 %fusion.59 = bf16[2,128,16,64]{1,3,2,0:T(8,128)(2,1)} fusion(bf16[2,1152,16,64]{1,3,2,0:T(8,128)(2,1)} %constant_dynamic-update-slice_fusion.36, f32[2,16,128,1152]{3,2,1,0:T(8,128)} %get-tuple-element.335, f32[2,16,128]{2,1,0:T(8,128)S(1)} %get-tuple-element.336), kind=kOutput, calls=%fused_computation.19.clone.1 | convolution fusion | flops 613679104 | bytes 24133632 | tf_op jit(solution)/shard_map/while/body/eval_jaxpr/ghqk,gkhd->gqhd/dot_general | solution.py:115
  257.8 4.0 reshape.431
  261.9 3.5 copy.142
  270.9 4.0 reshape.426
  274.9 3.5 copy.138
  278.5 4.0 reshape.432
  282.5 3.6 copy.143
  291.5 4.0 reshape.428
  295.5 3.5 copy.139
  299.1 4.0 reshape.433
  303.1 3.6 copy.144
  306.7 2.8 gather_fusion.7
  312.2 4.0 reshape.430
  316.3 3.5 copy.140
  319.8 4.0 reshape.434
  323.9 3.6 copy.145
  343.7 11.2 %fusion.58 = (f32[2,16,128]{2,1,0:T(8,128)S(1)}, f32[2,16,128,1152]{3,2,1,0:T(8,128)}) fusion(pred[2,1152]{1,0:T(4,128)(4,1)S(1)} %constant_dynamic-update-slice_fusion.41, bf16[2,1152,16,64]{1,3,2,0:T(8,128)(2,1)} %copy-done.8, bf16[6,128,16,64]{1,3,2,0:T(8,128)(2,1)} %get-tuple-element.387, s32[]{:T(128)S(6)} %select_n.121), kind=kOutput, calls=%fused_computation.97.clone.1 | convolution fusion | flops 622855296 | bytes 24135940 | tf_op jit(solution)/shard_map/while/body/eval_jaxpr/sub | solution.py:113
  354.9 12.4 %fusion.59 = bf16[2,128,16,64]{1,3,2,0:T(8,128)(2,1)} fusion(bf16[2,1152,16,64]{1,3,2,0:T(8,128)(2,1)} %constant_dynamic-update-slice_fusion.36, f32[2,16,128,1152]{3,2,1,0:T(8,128)} %get-tuple-element.335, f32[2,16,128]{2,1,0:T(8,128)S(1)} %get-tuple-element.336), kind=kOutput, calls=%fused_computation.19.clone.1 | convolution fusion | flops 613679104 | bytes 24133632 | tf_op jit(solution)/shard_map/while/body/eval_jaxpr/ghqk,gkhd->gqhd/dot_general | solution.py:115
  384.5 4.0 reshape.431
  388.6 3.5 copy.142
  397.5 4.0 reshape.426
  401.6 3.5 copy.138
  405.1 4.0 reshape.432
  409.2 3.6 copy.143
  418.2 4.0 reshape.428
  422.2 3.5 copy.139
  425.7 4.0 reshape.433
  429.8 3.6 copy.144
  433.4 2.8 gather_fusion.7
  438.9 4.0 reshape.430
  442.9 3.5 copy.140
  446.5 4.0 reshape.434
  450.5 3.6 copy.145
  470.4 11.2 %fusion.58 = (f32[2,16,128]{2,1,0:T(8,128)S(1)}, f32[2,16,128,1152]{3,2,1,0:T(8,128)}) fusion(pred[2,1152]{1,0:T(4,128)(4,1)S(1)} %constant_dynamic-update-slice_fusion.41, bf16[2,1152,16,64]{1,3,2,0:T(8,128)(2,1)} %copy-done.8, bf16[6,128,16,64]{1,3,2,0:T(8,128)(2,1)} %get-tuple-element.387, s32[]{:T(128)S(6)} %select_n.121), kind=kOutput, calls=%fused_computation.97.clone.1 | convolution fusion | flops 622855296 | bytes 24135940 | tf_op jit(solution)/shard_map/while/body/eval_jaxpr/sub | solution.py:113
  481.5 12.4 %fusion.59 = bf16[2,128,16,64]{1,3,2,0:T(8,128)(2,1)} fusion(bf16[2,1152,16,64]{1,3,2,0:T(8,128)(2,1)} %constant_dynamic-update-slice_fusion.36, f32[2,16,128,1152]{3,2,1,0:T(8,128)} %get-tuple-element.335, f32[2,16,128]{2,1,0:T(8,128)S(1)} %get-tuple-element.336), kind=kOutput, calls=%fused_computation.19.clone.1 | convolution fusion | flops 613679104 | bytes 24133632 | tf_op jit(solution)/shard_map/while/body/eval_jaxpr/ghqk,gkhd->gqhd/dot_general | solution.py:115
  499.2 4.8 fusion.30
  (238 shorter events, 145.7 us)
Async XLA Ops:
  0.0 499.2 %copy-start = (bf16[1024,1024]{1,0:T(8,128)(2,1)S(1)}, bf16[1024,1024]{1,0:T(8,128)(2,1)}, u32[]{:S(2)}) copy-start(bf16[1024,1024]{1,0:T(8,128)(2,1)} %param.15) | copy-start | bytes 6291460
  1.7 5.2 %collective-permute-start.6 = (s32[1]{0:T(128)}, s32[1]{0:T(128)}, u32[]{:S(2)}, u32[]{:S(2)}) collective-permute-start(s32[1]{0:T(128)} %get-tuple-element.196), channel_id=1, source_target_pairs={{14,0},{15,1},{0,2},{1,3},{2,4},{3,5},{4,6},{5,7},{6,8},{7,9},{8,1... | collective-permute-start | bytes 20 | tf_op jit(solution)/shard_map/ppermute | solution.py:14
  1.7 5.9 %collective-permute-start.4 = (s32[1]{0:T(128)}, s32[1]{0:T(128)}, u32[]{:S(2)}, u32[]{:S(2)}) collective-permute-start(s32[1]{0:T(128)} %get-tuple-element.197), channel_id=1, source_target_pairs={{2,0},{3,1},{4,2},{5,3},{6,4},{7,5},{8,6},{9,7},{10,8},{11,9},{12,... | collective-permute-start | bytes 20 | tf_op jit(solution)/shard_map/ppermute | solution.py:14
  3.2 5.0 collective-permute-start.2
  6.9 6.0 %collective-permute-start = (s32[1]{0:T(128)}, s32[1]{0:T(128)}, u32[]{:S(2)}, u32[]{:S(2)}) collective-permute-start(s32[1]{0:T(128)} %get-tuple-element.199), channel_id=1, source_target_pairs={{1,0},{2,1},{3,2},{4,3},{5,4},{6,5},{7,6},{8,7},{9,8},{10,9},{11,1... | collective-permute-start | bytes 20 | tf_op jit(solution)/shard_map/ppermute | solution.py:14
  13.5 8.5 %copy-start.7 = (bf16[1,768,1024]{2,1,0:T(8,128)(2,1)S(1)}, bf16[1,768,1024]{2,1,0:T(8,128)(2,1)}, u32[]{:S(2)}) copy-start(bf16[1,768,1024]{2,1,0:T(8,128)(2,1)} %param.13) | copy-start | bytes 4718596
  16.1 67.5 %copy-start.9 = (s32[1,4,6,2]{2,3,1,0:T(2,128)S(1)}, s32[1,4,6,2]{2,3,1,0:T(2,128)}, u32[]{:S(2)}) copy-start(s32[1,4,6,2]{2,3,1,0:T(2,128)} %param.18) | copy-start | bytes 580
  16.1 67.5 %copy-start.11 = (s32[1,4]{1,0:T(1,128)S(1)}, s32[1,4]{1,0:T(1,128)}, u32[]{:S(2)}) copy-start(s32[1,4]{1,0:T(1,128)} %param.16) | copy-start | bytes 52
  16.1 42.7 %collective-permute-start.11 = (bf16[384,1024]{1,0:T(8,128)(2,1)S(1)}, bf16[384,1024]{1,0:T(8,128)(2,1)}, u32[]{:S(2)}, u32[]{:S(2)}) collective-permute-start(bf16[384,1024]{1,0:T(8,128)(2,1)S(1)} %get-tuple-element.188), channel_id=1, source_target_pairs={{2,0},{3,1},{4,2},{5,3},{6,4},{7,5},{8,6},{9,7},{10,8},{11,9},{12,... | collective-permute-start | bytes 2359304 | tf_op jit(solution)/shard_map/ppermute | solution.py:14
  16.1 42.6 %collective-permute-start.9 = (bf16[384,1024]{1,0:T(8,128)(2,1)S(1)}, bf16[384,1024]{1,0:T(8,128)(2,1)}, u32[]{:S(2)}, u32[]{:S(2)}) collective-permute-start(bf16[384,1024]{1,0:T(8,128)(2,1)S(1)} %get-tuple-element.189), channel_id=1, source_target_pairs={{1,0},{2,1},{3,2},{4,3},{5,4},{6,5},{7,6},{8,7},{9,8},{10,9},{11,1... | collective-permute-start | bytes 2359304 | tf_op jit(solution)/shard_map/ppermute | solution.py:14
  16.2 47.0 %collective-permute-start.8 = (bf16[384,1024]{1,0:T(8,128)(2,1)S(1)}, bf16[384,1024]{1,0:T(8,128)(2,1)}, u32[]{:S(2)}, u32[]{:S(2)}) collective-permute-start(bf16[384,1024]{1,0:T(8,128)(2,1)S(1)} %get-tuple-element.190), channel_id=1, source_target_pairs={{15,0},{0,1},{1,2},{2,3},{3,4},{4,5},{5,6},{6,7},{7,8},{8,9},{9,10... | collective-permute-start | bytes 2359304 | tf_op jit(solution)/shard_map/ppermute | solution.py:14
  20.6 79.4 %collective-permute-start.10 = (bf16[384,1024]{1,0:T(8,128)(2,1)S(1)}, bf16[384,1024]{1,0:T(8,128)(2,1)}, u32[]{:S(2)}, u32[]{:S(2)}) collective-permute-start(bf16[384,1024]{1,0:T(8,128)(2,1)S(1)} %get-tuple-element.191), channel_id=1, source_target_pairs={{14,0},{15,1},{0,2},{1,3},{2,4},{3,5},{4,6},{5,7},{6,8},{7,9},{8,1... | collective-permute-start | bytes 2359304 | tf_op jit(solution)/shard_map/ppermute | solution.py:14
  23.8 76.2 %collective-permute-start.7 = (bf16[384,1024]{1,0:T(8,128)(2,1)}, bf16[384,1024]{1,0:T(8,128)(2,1)}, u32[]{:S(2)}, u32[]{:S(2)}) collective-permute-start(bf16[384,1024]{1,0:T(8,128)(2,1)} %get-tuple-element.192), channel_id=1, source_target_pairs={{2,0},{3,1},{4,2},{5,3},{6,4},{7,5},{8,6},{9,7},{10,8},{11,9},{12,... | collective-permute-start | bytes 2359304 | tf_op jit(solution)/shard_map/ppermute | solution.py:14
  58.8 41.2 %collective-permute-start.3 = (bf16[384,1024]{1,0:T(8,128)(2,1)}, bf16[384,1024]{1,0:T(8,128)(2,1)}, u32[]{:S(2)}, u32[]{:S(2)}) collective-permute-start(bf16[384,1024]{1,0:T(8,128)(2,1)} %get-tuple-element.193), channel_id=1, source_target_pairs={{1,0},{2,1},{3,2},{4,3},{5,4},{6,5},{7,6},{8,7},{9,8},{10,9},{11,1... | collective-permute-start | bytes 2359304 | tf_op jit(solution)/shard_map/ppermute | solution.py:14
  58.8 41.2 %collective-permute-start.1 = (bf16[384,1024]{1,0:T(8,128)(2,1)}, bf16[384,1024]{1,0:T(8,128)(2,1)}, u32[]{:S(2)}, u32[]{:S(2)}) collective-permute-start(bf16[384,1024]{1,0:T(8,128)(2,1)} %get-tuple-element.194), channel_id=1, source_target_pairs={{15,0},{0,1},{1,2},{2,3},{3,4},{4,5},{5,6},{6,7},{7,8},{8,9},{9,10... | collective-permute-start | bytes 2359304 | tf_op jit(solution)/shard_map/ppermute | solution.py:14
  63.2 55.9 %collective-permute-start.5 = (bf16[384,1024]{1,0:T(8,128)(2,1)}, bf16[384,1024]{1,0:T(8,128)(2,1)}, u32[]{:S(2)}, u32[]{:S(2)}) collective-permute-start(bf16[384,1024]{1,0:T(8,128)(2,1)} %get-tuple-element.195), channel_id=1, source_target_pairs={{14,0},{15,1},{0,2},{1,3},{2,4},{3,5},{4,6},{5,7},{6,8},{7,9},{8,1... | collective-permute-start | bytes 2359304 | tf_op jit(solution)/shard_map/ppermute | solution.py:14
  83.9 10.2 %copy-start.10 = (s32[1,4,6]{2,1,0:T(4,128)S(1)}, s32[1,4,6]{2,1,0:T(4,128)}, u32[]{:S(2)}) copy-start(s32[1,4,6]{2,1,0:T(4,128)} %param.19) | copy-start | bytes 292
  207.2 4.1 copy-start.4
  207.2 4.3 copy-start.5
  207.2 4.4 copy-start.6
  209.8 3.8 copy-start.1
  211.3 3.6 copy-start.2
  211.4 4.5 copy-start.3
  211.6 4.4 copy-start.8
  333.8 4.1 copy-start.4
  333.8 4.3 copy-start.5
  333.8 4.4 copy-start.6
  336.4 3.8 copy-start.1
  337.9 3.6 copy-start.2
  338.1 4.5 copy-start.3
  338.2 4.4 copy-start.8
  460.4 4.1 copy-start.4
  460.5 4.3 copy-start.5
  460.5 4.4 copy-start.6
  463.1 3.8 copy-start.1
  464.6 3.6 copy-start.2
  464.7 4.5 copy-start.3
  464.9 4.4 copy-start.8
where the time goes:
time: 508 us; the launch traced here: 504 us
  local copies, waits for them, and re-layouts  321 us (63%)
  matrix products  75.3 us (15%)
  waiting for transfers between devices  64 us (13%)
  starting transfers between devices  36 us (7%)
    concatenate x27, local copies, waits for them, and re-layouts, one_group(): jnp.concatenate(key_parts, axis=1).reshape(group_size, -1, HEADS, head_dim)  91.6 us
    concatenate x27, local copies, waits for them, and re-layouts, one_group(): jnp.concatenate(value_parts, axis=1)  86.8 us
    ppermute x12, waiting for transfers between devices, passed_along(): return lax.ppermute(block, axis, route)  64 us
    dot_general x3, matrix products, one_group(): jnp.einsum('ghqk,gkhd->gqhd', weights, value_group, preferred_element_typ...  37.1 us
    ppermute x12, starting transfers between devices, passed_along(): return lax.ppermute(block, axis, route)  36 us
    sub x3, matrix products, one_group(): expo_scores = jnp.exp(scores - row_max)  33.4 us
    gather x12, local copies, waits for them, and re-layouts, one_group(): key_tiles[source][block_index]  32.9 us
    gather x12, local copies, waits for them, and re-layouts, one_group(): value_tiles[source][block_index]  29.7 us
  transfers between devices with their start and end apart: 12, of which 4 were waited for; matrix products, arithmetic and copies ran while one was open for 2% of the time, Pallas kernels for 0%

commit v1 on v0

v1 whole, which is shorter than its diff:
```python
import functools
import math

import jax
import jax.numpy as jnp
from jax import lax
from jax.experimental import pallas as pl
from jax.experimental.pallas import tpu as pltpu
from jax.sharding import PartitionSpec as P

HEADS = 16
LANES = 128
ROLES = 4
HIDDEN = -1e30


def kernel(cfg, q_hbm, k_hbm, v_hbm, near_ref, start_ref, block_ref, count_ref, out_ref, *scratch):
    cameras, rigs, chunks, qblocks, most, head_dim = cfg
    relay = rigs == 1 and cameras % 4 == 0
    buffers = [scratch[r * chunks:(r + 1) * chunks] for r in range(ROLES)]
    q_ref, k_ref, v_ref, own_sem, first_send, first_recv, next_send, next_recv = scratch[ROLES * chunks:]
    part_a, part_b, part_x, part_z = range(ROLES)
    block_len = q_ref.shape[1]
    me = lax.axis_index("cam")

    def at(offset):
        return lax.rem(me + offset + 2 * cameras, cameras)

    if relay:
        column = lax.rem(me // 2, 2)
        core = lax.rem(me, 2)
        partner = me + 1 - 2 * core
        across = me + 2 - 4 * column
        z_to = at(4 - 8 * column)
        z_from = at(8 * column - 4)
        from_x = lax.rem(column + core, 2) == 0
        z_view = at(4 * column - 2)
        partner_x = partner + 2 - 4 * column
        partner_z = lax.rem(partner + 4 * column - 2 + cameras, cameras)
        b_view = jnp.where(from_x, partner_z, partner_x)
        views = (partner, b_view, across, z_view)
        peers = (partner, across, z_to, z_from)
        first = ((part_x, across), (part_a, partner))
    else:
        views = (at(rigs), at(-rigs), at(2 * rigs), at(-2 * rigs))
        peers = views
        first = (
            (part_a, views[1]), (part_b, views[0]), (part_x, views[3]), (part_z, views[2])
        )

    own_copies = [
        pltpu.make_async_copy(src, dst, own_sem.at[n])
        for n, (src, dst) in enumerate(((q_hbm, q_ref), (k_hbm, k_ref), (v_hbm, v_ref)))
    ]
    for copy in own_copies:
        copy.start()
    barrier = pltpu.get_barrier_semaphore()
    for peer in peers:
        pl.semaphore_signal(
            barrier, inc=1, device_id={"cam": peer}, device_id_type=pl.DeviceIdType.MESH
        )
    pl.semaphore_wait(barrier, len(peers))

    def first_copy(lane, g, kind):
        role, target = first[lane]
        source = (k_hbm, v_hbm)[kind]
        return pltpu.make_async_remote_copy(
            src_ref=source.at[:, :, pl.ds(g * LANES, LANES)],
            dst_ref=buffers[role][g].at[kind],
            send_sem=first_send.at[lane, g, kind],
            recv_sem=first_recv.at[lane, g, kind],
            device_id={"cam": target},
            device_id_type=pl.DeviceIdType.MESH,
        )

    def next_copy(role, g, source_role, target):
        return pltpu.make_async_remote_copy(
            src_ref=buffers[source_role][g],
            dst_ref=buffers[role][g],
            send_sem=next_send.at[role // 2, g],
            recv_sem=next_recv.at[role // 2, g],
            device_id={"cam": target},
            device_id_type=pl.DeviceIdType.MESH,
        )

    for lane in range(len(first)):
        for g in range(chunks):
            for kind in range(2):
                first_copy(lane, g, kind).start()

    def first_wait(lane, g):
        for kind in range(2):
            first_copy(lane, g, kind).wait_recv()

    slots = []
    for view in views:
        slot = jnp.int32(0)
        for s in range(1, ROLES):
            slot = jnp.where(near_ref[0, s] == view, s, slot)
        slots.append(slot)
    starts = [start_ref[0, slot] for slot in slots]

    def compute(g):
        cols = slice(g * LANES, (g + 1) * LANES)

        def one_block(b, carry):
            heads = LANES // head_dim
            q = q_ref[b, :, cols] * jnp.asarray(1.0 / math.sqrt(head_dim), jnp.bfloat16)
            lane = lax.broadcasted_iota(jnp.int32, (block_len, LANES), 1) // head_dim
            q2 = jnp.concatenate(
                [jnp.where(lane == h, q, jnp.zeros_like(q)) for h in range(heads)], axis=0
            )
            dims = (((1,), (1,)), ((), ()))
            scores = [
                lax.dot_general(q2, k_ref[b, :, cols], dims, preferred_element_type=jnp.float32)
            ]
            vals = [v_ref[b, :, cols]]
            for r in range(ROLES):
                buffer = buffers[r][g]
                key_parts, val_parts, bias = [], [], []
                live = count_ref[0, slots[r], b]
                for m in range(most):
                    near = starts[r] + block_ref[0, slots[r], b, m]
                    if m > 0:
                        near = jnp.where(m < live, near, 0)
                        bias.append(jnp.where(m < live, 0.0, HIDDEN))
                    key_parts.append(buffer[0, near])
                    val_parts.append(buffer[1, near])
                got = lax.dot_general(
                    q2,
                    jnp.concatenate(key_parts, axis=0),
                    dims,
                    preferred_element_type=jnp.float32,
                )
                pieces = [got[:, :block_len]]
                for m in range(1, most):
                    pieces.append(got[:, m * block_len:(m + 1) * block_len] + bias[m - 1])
                scores.append(jnp.concatenate(pieces, axis=1))
                vals.append(jnp.concatenate(val_parts, axis=0))
            all_scores = jnp.concatenate(scores, axis=1)
            top = jnp.max(all_scores, axis=1, keepdims=True)
            expo = jnp.exp(all_scores - top)
            total = jnp.sum(expo, axis=1, keepdims=True)
            mixed = jnp.dot(
                expo.astype(jnp.bfloat16),
                jnp.concatenate(vals, axis=0),
                preferred_element_type=jnp.float32,
            )
            mixed = mixed / total
            result = mixed[:block_len]
            for h in range(1, heads):
                result = jnp.where(lane == h, mixed[h * block_len:(h + 1) * block_len], result)
            out_ref[b, :, cols] = result.astype(out_ref.dtype)
            return carry

        lax.fori_loop(0, qblocks, one_block, 0)

    if relay:

        def z_send(g):
            return next_copy(part_z, g, part_x, z_to)

        def b_send(g, source):
            return next_copy(part_b, g, source, partner)

        def after_x(g):
            first_wait(0, g)
            z_send(g).start()

            @pl.when(from_x)
            def _():
                b_send(g, part_x).start()

        def after_z(g):
            z_send(g).wait_recv()

            @pl.when(jnp.logical_not(from_x))
            def _():
                b_send(g, part_z).start()

        def finish(g):
            first_wait(1, g)
            b_send(g, part_x).wait_recv()
            compute(g)

        for step in range(chunks):
            after_x(step)
            if step >= 1:
                after_z(step - 1)
            if step == 1:
                for copy in own_copies:
                    copy.wait()
            if step >= 2:
                finish(step - 2)
        if chunks >= 2:
            finish(chunks - 2)
        else:
            for copy in own_copies:
                copy.wait()
        after_z(chunks - 1)
        finish(chunks - 1)
        for g in range(chunks):
            z_send(g).wait_send()

            @pl.when(from_x)
            def _():
                b_send(g, part_x).wait_send()

            @pl.when(jnp.logical_not(from_x))
            def _():
                b_send(g, part_z).wait_send()
    else:
        for copy in own_copies:
            copy.wait()
        for g in range(chunks):
            for lane in range(len(first)):
                first_wait(lane, g)
            compute(g)
    for lane in range(len(first)):
        for g in range(chunks):
            for kind in range(2):
                first_copy(lane, g, kind).wait_send()


def per_device(
    queries, keys, values, residual, w_out, neighbours, band_start, band_blocks, band_count
):
    tokens, width = queries.shape[1:]
    qblocks = band_count.shape[2]
    most = band_blocks.shape[3]
    cameras = lax.axis_size("cam")
    rigs = cameras // min(32, cameras)
    chunks = width // LANES
    cfg = (cameras, rigs, chunks, qblocks, most, width // HEADS)
    lanes = 2 if rigs == 1 and cameras % 4 == 0 else 4
    dma = pltpu.SemaphoreType.DMA
    anywhere = pl.BlockSpec(memory_space=pl.ANY)
    scalars = pl.BlockSpec(memory_space=pltpu.SMEM)
    blocks = (qblocks, tokens // qblocks, width)
    attended = pl.pallas_call(
        functools.partial(kernel, cfg),
        out_shape=jax.ShapeDtypeStruct(blocks, jnp.bfloat16),
        in_specs=[anywhere] * 3 + [scalars] * 4,
        out_specs=pl.BlockSpec(memory_space=pltpu.VMEM),
        scratch_shapes=[pltpu.VMEM((2,) + blocks[:2] + (LANES,), jnp.bfloat16)] * (ROLES * chunks)
        + [pltpu.VMEM(blocks, jnp.bfloat16)] * 3
        + [
            dma((3,)),
            dma((lanes, chunks, 2)),
            dma((lanes, chunks, 2)),
            dma((2, chunks)),
            dma((2, chunks)),
        ],
        compiler_params=pltpu.CompilerParams(
            collective_id=0, has_side_effects=True, vmem_limit_bytes=48 * 1024 * 1024
        ),
        name="band_attention",
    )(*(x[0].reshape(blocks) for x in (queries, keys, values)), neighbours, band_start, band_blocks, band_count)
    result = residual[0].astype(jnp.float32) + jnp.dot(
        attended.reshape(tokens, width), w_out, preferred_element_type=jnp.float32
    )
    return result.astype(jnp.bfloat16)[None]


def solution(mesh):
    rows = ("scene", "cam")
    return jax.shard_map(
        per_device,
        mesh=mesh,
        in_specs=(
            P(rows, None, None),
            P(rows, None, None),
            P(rows, None, None),
            P(rows, None, None),
            P(),
            P(rows, None),
            P(rows, None),
            P(rows, None, None, None),
            P(rows, None, None),
        ),
        out_specs=P(rows, None, None),
        check_vma=False,
    )
```

time: 508 us -> 100 us (0.20)
  the two profiles are of different devices: /device:TPU:31 before, /device:TPU:0 now
where the time goes in v1:
time: 100 us; the launch traced here: 99.7 us
  Pallas kernels  91 us (91%)
  local copies, waits for them, and re-layouts  5.75 us (6%)
  matrix products  2.97 us (3%)
    pallas_call x1, Pallas kernels, per_device(): pl.pallas_call(functools.partial(kernel, cfg), out_shape=jax.ShapeDtypeSt...  91 us
    unnamed x15, local copies, waits for them, and re-layouts  5.75 us
    dot_general x1, matrix products, per_device(): jnp.dot(attended.reshape(tokens, width), w_out, preferred_element_type=jn...  2.97 us

profile of v1, /device:TPU:0, one launch (start us, length us, event | category | flops | bytes accessed | tf_op | source)
XLA Modules:
  0.0 99.7 jit_solution(9836089436970458279)
XLA Ops:
  0.0 0.0 copy-start
  0.0 0.9 copy.10.block_ref
  0.9 0.0 copy-start.1
  0.9 1.4 %copy-done.1 = bf16[1,768,1024]{2,1,0:T(8,128)(2,1)S(1)} copy-done((bf16[1,768,1024]{2,1,0:T(8,128)(2,1)S(1)}, bf16[1,768,1024]{2,1,0:T(8,128)(2,1)}, u32[]{:S(2)}) %copy-start.1) | copy-done | bytes 1572888
  2.4 0.0 copy-start.2
  2.4 1.4 %copy-done.2 = bf16[1,768,1024]{2,1,0:T(8,128)(2,1)S(1)} copy-done((bf16[1,768,1024]{2,1,0:T(8,128)(2,1)S(1)}, bf16[1,768,1024]{2,1,0:T(8,128)(2,1)}, u32[]{:S(2)}) %copy-start.2) | copy-done | bytes 1572888
  3.8 0.0 copy-start.3
  3.8 0.7 copy-done.3
  4.4 0.0 copy-start.4
  4.4 0.7 copy-done.4
  5.1 0.0 copy-start.5
  5.1 0.7 copy-done.5
  5.8 0.0 copy-start.6
  5.8 91.0 %band_attention.1 = bf16[6,128,1024]{2,1,0:T(8,128)(2,1)S(1)} custom-call(bf16[6,128,1024]{2,1,0:T(8,128)(2,1)S(1)} %bitcast.13, bf16[6,128,1024]{2,1,0:T(8,128)(2,1)S(1)} %bitcast.14, bf16[6,128,1024]{2,1,0:T(8,128)(2,1)} %bitcast.16, s32[1,4]{1,0:T(1,128)S(1)} %copy-done.4, s32[1,4]{1,0:T(1,128)S(1)} %copy-done.5, s32[1,4,6,2]{3,2,1,0:T(8,128)S(1)} %copy.10.block_ref, ...), custom_call_target="tpu_custom_call" | custom-call | tf_op jit(solution)/shard_map/band_attention/pallas_call | solution.py:240
  96.7 0.0 copy-done
  96.8 0.0 copy-done.6
  96.8 3.0 %fusion.1 = bf16[1,768,1024]{2,1,0:T(8,128)(2,1)} fusion(bf16[768,1024]{1,0:T(8,128)(2,1)S(1)} %bitcast.15, bf16[1024,1024]{1,0:T(8,128)(2,1)S(1)} %copy-done, bf16[1,768,1024]{2,1,0:T(8,128)(2,1)S(1)} %copy-done.6), kind=kOutput, calls=%fused_computation.2 | convolution fusion | flops 1612972032 | bytes 6815744 | tf_op jit(solution)/shard_map/dot_general | solution.py:259
Async XLA Ops:
  0.0 96.7 %copy-start = (bf16[1024,1024]{1,0:T(8,128)(2,1)S(1)}, bf16[1024,1024]{1,0:T(8,128)(2,1)}, u32[]{:S(2)}) copy-start(bf16[1024,1024]{1,0:T(8,128)(2,1)} %param.13) | copy-start | bytes 6291460
  0.9 1.4 %copy-start.1 = (bf16[1,768,1024]{2,1,0:T(8,128)(2,1)S(1)}, bf16[1,768,1024]{2,1,0:T(8,128)(2,1)}, u32[]{:S(2)}) copy-start(bf16[1,768,1024]{2,1,0:T(8,128)(2,1)} %param.9) | copy-start | bytes 4718596
  2.4 1.4 %copy-start.2 = (bf16[1,768,1024]{2,1,0:T(8,128)(2,1)S(1)}, bf16[1,768,1024]{2,1,0:T(8,128)(2,1)}, u32[]{:S(2)}) copy-start(bf16[1,768,1024]{2,1,0:T(8,128)(2,1)} %param.10) | copy-start | bytes 4718596
  3.8 0.7 copy-start.3
  4.4 0.7 copy-start.4
  5.1 0.7 copy-start.5
  5.8 91.0 %copy-start.6 = (bf16[1,768,1024]{2,1,0:T(8,128)(2,1)S(1)}, bf16[1,768,1024]{2,1,0:T(8,128)(2,1)}, u32[]{:S(2)}) copy-start(bf16[1,768,1024]{2,1,0:T(8,128)(2,1)} %param.12) | copy-start | bytes 4718596

commit v2 on v1

--- a/solution.py
+++ b/solution.py
@@ -14,9 +14,13 @@
 HIDDEN = -1e30
 
 
+def relays(cameras, rigs, qblocks):
+    return rigs == 1 and cameras % 4 == 0 and qblocks % 2 == 0
+
+
 def kernel(cfg, q_hbm, k_hbm, v_hbm, near_ref, start_ref, block_ref, count_ref, out_ref, *scratch):
     cameras, rigs, chunks, qblocks, most, head_dim = cfg
-    relay = rigs == 1 and cameras % 4 == 0
+    relay = relays(cameras, rigs, qblocks)
     buffers = [scratch[r * chunks:(r + 1) * chunks] for r in range(ROLES)]
     q_ref, k_ref, v_ref, own_sem, first_send, first_recv, next_send, next_recv = scratch[ROLES * chunks:]
     part_a, part_b, part_x, part_z = range(ROLES)
@@ -61,36 +65,50 @@
         )
     pl.semaphore_wait(barrier, len(peers))
 
-    def first_copy(lane, g, kind):
+    def first_copy(lane, g, kind, rows):
         role, target = first[lane]
-        source = (k_hbm, v_hbm)[kind]
+        source = (v_hbm if isinstance(kind, int) and kind == 1 else k_hbm)
+        part = kind * (qblocks // rows.size) + rows.start // rows.size
         return pltpu.make_async_remote_copy(
-            src_ref=source.at[:, :, pl.ds(g * LANES, LANES)],
-            dst_ref=buffers[role][g].at[kind],
-            send_sem=first_send.at[lane, g, kind],
-            recv_sem=first_recv.at[lane, g, kind],
+            src_ref=source.at[rows, :, pl.ds(g * LANES, LANES)],
+            dst_ref=buffers[role][g].at[kind, rows],
+            send_sem=first_send.at[lane, g, part],
+            recv_sem=first_recv.at[lane, g, part],
             device_id={"cam": target},
             device_id_type=pl.DeviceIdType.MESH,
         )
 
-    def next_copy(role, g, source_role, target):
+    def next_copy(role, g, source_role, target, part):
+        kind, rows = piece(part)
         return pltpu.make_async_remote_copy(
-            src_ref=buffers[source_role][g],
-            dst_ref=buffers[role][g],
-            send_sem=next_send.at[role // 2, g],
-            recv_sem=next_recv.at[role // 2, g],
+            src_ref=buffers[source_role][g].at[kind, rows],
+            dst_ref=buffers[role][g].at[kind, rows],
+            send_sem=next_send.at[role // 2, g, part],
+            recv_sem=next_recv.at[role // 2, g, part],
             device_id={"cam": target},
             device_id_type=pl.DeviceIdType.MESH,
         )
 
+    splits = qblocks // 2 if relay else 1
+
+    def piece(part):
+        return part // splits, pl.ds((part % splits) * (qblocks // splits), qblocks // splits)
+
+    whole = pl.ds(0, qblocks)
+
+    def first_parts(lane):
+        if relay and lane == 0:
+            return [piece(part) for part in range(2 * splits)]
+        return [(kind, whole) for kind in range(2)]
+
     for lane in range(len(first)):
         for g in range(chunks):
-            for kind in range(2):
-                first_copy(lane, g, kind).start()
+            for kind, rows in first_parts(lane):
+                first_copy(lane, g, kind, rows).start()
 
     def first_wait(lane, g):
-        for kind in range(2):
-            first_copy(lane, g, kind).wait_recv()
+        for kind, rows in first_parts(lane):
+            first_copy(lane, g, kind, rows).wait_recv()
 
     slots = []
     for view in views:
@@ -100,7 +118,7 @@
         slots.append(slot)
     starts = [start_ref[0, slot] for slot in slots]
 
-    def compute(g):
+    def block_of(g):
         cols = slice(g * LANES, (g + 1) * LANES)
 
         def one_block(b, carry):
@@ -153,73 +171,91 @@
             out_ref[b, :, cols] = result.astype(out_ref.dtype)
             return carry
 
-        lax.fori_loop(0, qblocks, one_block, 0)
+        return one_block
+
+    def compute(g, unroll):
+        lax.fori_loop(0, qblocks, block_of(g), 0, unroll=unroll)
 
     if relay:
 
-        def z_send(g):
-            return next_copy(part_z, g, part_x, z_to)
-
-        def b_send(g, source):
-            return next_copy(part_b, g, source, partner)
-
-        def after_x(g):
-            first_wait(0, g)
-            z_send(g).start()
+        def z_send(g, part):
+            return next_copy(part_z, g, part_x, z_to, part)
+
+        def b_send(g, source, part):
+            return next_copy(part_b, g, source, partner, part)
+
+        def after_x(g, part):
+            first_copy(0, g, *piece(part)).wait_recv()
+            z_send(g, part).start()
 
             @pl.when(from_x)
             def _():
-                b_send(g, part_x).start()
-
-        def after_z(g):
-            z_send(g).wait_recv()
+                b_send(g, part_x, part).start()
+
+        def after_z(g, part):
+            z_send(g, part).wait_recv()
 
             @pl.when(jnp.logical_not(from_x))
             def _():
-                b_send(g, part_z).start()
-
-        def finish(g):
+                b_send(g, part_z, part).start()
+
+        def arrive(g):
             first_wait(1, g)
-            b_send(g, part_x).wait_recv()
-            compute(g)
-
-        for step in range(chunks):
-            after_x(step)
-            if step >= 1:
-                after_z(step - 1)
-            if step == 1:
+
+            def one_part(part, carry):
+                b_send(g, part_x, part).wait_recv()
+                return carry
+
+            lax.fori_loop(0, qblocks, one_part, 0)
+
+        for step in range(chunks + 1):
+            if step == 2 or step == chunks < 2:
                 for copy in own_copies:
                     copy.wait()
-            if step >= 2:
-                finish(step - 2)
-        if chunks >= 2:
-            finish(chunks - 2)
-        else:
-            for copy in own_copies:
-                copy.wait()
-        after_z(chunks - 1)
-        finish(chunks - 1)
+            done = step - 2 if step < chunks else chunks - 2
+            if done >= 0:
+                arrive(done)
+
+            def one_part(part, carry):
+                if step < chunks:
+                    after_x(step, part)
+                if step >= 1:
+                    after_z(step - 1, part)
+                if done >= 0:
+                    block_of(done)(part, carry)
+                return carry
+
+            lax.fori_loop(0, qblocks, one_part, 0)
+        arrive(chunks - 1)
+        compute(chunks - 1, 3 if qblocks % 3 == 0 else 1)
+
         for g in range(chunks):
-            z_send(g).wait_send()
-
-            @pl.when(from_x)
-            def _():
-                b_send(g, part_x).wait_send()
-
-            @pl.when(jnp.logical_not(from_x))
-            def _():
-                b_send(g, part_z).wait_send()
+
+            def one_part(part, carry):
+                z_send(g, part).wait_send()
+
+                @pl.when(from_x)
+                def _():
+                    b_send(g, part_x, part).wait_send()
+
+                @pl.when(jnp.logical_not(from_x))
+                def _():
+                    b_send(g, part_z, part).wait_send()
+
+                return carry
+
+            lax.fori_loop(0, qblocks, one_part, 0)
     else:
         for copy in own_copies:
             copy.wait()
         for g in range(chunks):
             for lane in range(len(first)):
                 first_wait(lane, g)
-            compute(g)
+            compute(g, 1)
     for lane in range(len(first)):
         for g in range(chunks):
-            for kind in range(2):
-                first_copy(lane, g, kind).wait_send()
+            for kind, rows in first_parts(lane):
+                first_copy(lane, g, kind, rows).wait_send()
 
 
 def per_device(
@@ -232,7 +268,7 @@
     rigs = cameras // min(32, cameras)
     chunks = width // LANES
     cfg = (cameras, rigs, chunks, qblocks, most, width // HEADS)
-    lanes = 2 if rigs == 1 and cameras % 4 == 0 else 4
+    lanes = 2 if relays(cameras, rigs, qblocks) else 4
     dma = pltpu.SemaphoreType.DMA
     anywhere = pl.BlockSpec(memory_space=pl.ANY)
     scalars = pl.BlockSpec(memory_space=pltpu.SMEM)
@@ -246,13 +282,13 @@
         + [pltpu.VMEM(blocks, jnp.bfloat16)] * 3
         + [
             dma((3,)),
-            dma((lanes, chunks, 2)),
-            dma((lanes, chunks, 2)),
-            dma((2, chunks)),
-            dma((2, chunks)),
+            dma((lanes, chunks, max(2, qblocks))),
+            dma((lanes, chunks, max(2, qblocks))),
+            dma((2, chunks, qblocks)),
+            dma((2, chunks, qblocks)),
         ],
         compiler_params=pltpu.CompilerParams(
-            collective_id=0, has_side_effects=True, vmem_limit_bytes=48 * 1024 * 1024
+            collective_id=0, has_side_effects=True, vmem_limit_bytes=62 * 1024 * 1024
         ),
         name="band_attention",
     )(*(x[0].reshape(blocks) for x in (queries, keys, values)), neighbours, band_start, band_blocks, band_count)

time: 100 us -> 96.5 us (0.965)
  local copies, waits for them, and re-layouts: 5.75 us -> 1.39 us
  matrix products: 2.97 us -> 5.01 us
  Pallas kernels: 91 us -> 89.9 us
    unnamed x15 -> x3, local copies, waits for them, and re-layouts: 5.75 us -> 1.39 us
    dot_general x1, matrix products: 2.97 us -> 5.01 us  [per_device(): jnp.dot(attended.reshape(tokens, width), w_out, preferred_element_type=jn...]
    pallas_call x1, Pallas kernels: 91 us -> 89.9 us  [per_device(): pl.pallas_call(functools.partial(kernel, cfg), out_shape=jax.ShapeDtypeSt...]
where the time goes in v2:
time: 96.5 us; the launch traced here: 96.3 us
  Pallas kernels  89.9 us (93%)
  matrix products  5.01 us (5%)
  local copies, waits for them, and re-layouts  1.39 us (1%)
    pallas_call x1, Pallas kernels, per_device(): pl.pallas_call(functools.partial(kernel, cfg), out_shape=jax.ShapeDtypeSt...  89.9 us
    dot_general x1, matrix products, per_device(): jnp.dot(attended.reshape(tokens, width), w_out, preferred_element_type=jn...  5.01 us

profile of v2, /device:TPU:0, one launch (start us, length us, event | category | flops | bytes accessed | tf_op | source)
XLA Modules:
  0.0 96.3 jit_solution(17552824077744069526)
XLA Ops:
  0.0 1.4 %copy.10.block_ref = s32[1,4,6,2]{3,2,1,0:T(8,128)} copy(s32[1,4,6,2]{2,3,1,0:T(2,128)} %param.16) | data formatting | bytes 384 | tf_op args[7]
  1.4 0.0 copy-start
  1.4 89.9 %band_attention.1 = bf16[6,128,1024]{2,1,0:T(8,128)(2,1)} custom-call(bf16[6,128,1024]{2,1,0:T(8,128)(2,1)} %bitcast.13, bf16[6,128,1024]{2,1,0:T(8,128)(2,1)} %bitcast.14, bf16[6,128,1024]{2,1,0:T(8,128)(2,1)} %bitcast.15, s32[1,4]{1,0:T(1,128)} %near_ref.1, s32[1,4]{1,0:T(1,128)} %start_ref.1, s32[1,4,6,2]{3,2,1,0:T(8,128)} %copy.10.block_ref, ...), custom_call_target="tpu_custom_call" | custom-call | tf_op jit(solution)/shard_map/band_attention/pallas_call | solution.py:276
  91.3 0.0 copy-done
  91.3 5.0 %fusion.1 = bf16[1,768,1024]{2,1,0:T(8,128)(2,1)} fusion(bf16[768,1024]{1,0:T(8,128)(2,1)} %bitcast.16, bf16[1024,1024]{1,0:T(8,128)(2,1)} %param.13, bf16[1,768,1024]{2,1,0:T(8,128)(2,1)S(1)} %copy-done), kind=kOutput, calls=%fused_computation.2 | convolution fusion | flops 1612972032 | bytes 6815744 | tf_op jit(solution)/shard_map/dot_general | solution.py:295
Async XLA Ops:
  1.4 89.9 %copy-start = (bf16[1,768,1024]{2,1,0:T(8,128)(2,1)S(1)}, bf16[1,768,1024]{2,1,0:T(8,128)(2,1)}, u32[]{:S(2)}) copy-start(bf16[1,768,1024]{2,1,0:T(8,128)(2,1)} %param.12) | copy-start | bytes 4718596
